TPU v7x, 768 devices: a whole 4x8x12 slice. The times are simulated.
768 devices in a mesh: lon: 16 (over x, z_hi), lat: 48 (over z_lo, y, core).
Axes of the slice: x: 4, y: 8, z: 12 (z_hi: 4, z_lo: 3; z = z_hi * 3 + z_lo), core: 2. Of those that a mesh axis runs over, the one named last changes fastest.
Arguments:
- spectrum: float32 [128, 3072, 648], P('lon', 'lat'), may hold values from 0.01 to 1
- sea_mask: int32 [128, 3072], P('lon', 'lat'), may hold values from 0 to 1, as said below
- ice_flags: int32 [128, 3072], P('lon', 'lat'), may hold values 0 or 1
- wind_forcing: float32 [128, 3072], P('lon', 'lat'), may hold values from 0.1 to 1.5
- group_speed: float32 [18], replicated, may hold values from 0.3 to 1
- coupling: bfloat16 [648, 648], replicated, may hold values from -0.25 to 0.25
Outputs:
- field: float32 [128, 3072, 648], P('lon', 'lat')
Inputs may be any that keep to these rules, and one draw needn't show every extreme that they name: `sea_mask`: each device's block of 8 x 64 cells holds at most 384 sea cells and at least 128; in every draw some block holds exactly 384.
All inputs are finite; a program needn't handle non-finite values. No bound on the sum of `ice_flags` on one device may be relied on, other than what follows from the above.
Results may differ from a plain program's by a relative error of at most 0.00079.
Values sent between devices are 32-bit elements; how exact they have to be, the bound alone decides.
A program may use at most 32 MiB of HBM per device.

v0:
```python
import math

import jax
import jax.numpy as jnp
from jax import lax
from jax.sharding import PartitionSpec as P

DIRS = 36
STEPS = 4


time_step = 0.2
dissipation = 0.5


def extended(value, sides, width, wrap):
    for axis, dim in sides:
        size, length = (lax.axis_size(axis), value.shape[dim])
        up = [(i, (i + 1) % size) for i in range(size if wrap else size - 1)]
        down = [(j, i) for i, j in up]
        last = lax.slice_in_dim(value, length - width, length, axis=dim)
        first = lax.slice_in_dim(value, 0, width, axis=dim)
        before = lax.ppermute(last, axis, up)
        after = lax.ppermute(first, axis, down)
        value = jnp.concatenate([before, value, after], axis=dim)
    return value


def speed_tables(rows, total_rows, group_speed, dirs):
    theta = (jnp.arange(dirs).astype(jnp.float32) + 0.5) * (2.0 * math.pi / dirs)
    latitude = (-60.0 + 120.0 * (rows.astype(jnp.float32) + 0.5) / total_rows) * (math.pi / 180.0)
    scaled = jnp.outer(jnp.cos(theta), group_speed).reshape(-1)
    along_x = (0.225 * scaled)[None, :] / jnp.cos(latitude)[:, None]
    along_y = 0.45 * jnp.outer(jnp.sin(theta), group_speed).reshape(-1)
    return (along_x, along_y)


def upwind(field, west, east, south, north, along_x, along_y):
    speed_x = along_x[None]
    result = (
        field
        - jnp.maximum(speed_x, 0.0) * (field - west)
        - jnp.minimum(speed_x, 0.0) * (east - field)
    )
    return (
        result
        - jnp.maximum(along_y, 0.0) * (field - south)
        - jnp.minimum(along_y, 0.0) * (north - field)
    )


def sources(advected, wind_forcing, ice_flags, coupling):
    shape = advected.shape
    energy = jnp.mean(advected, axis=-1, keepdims=True)
    flat = advected.reshape(-1, shape[-1]).astype(jnp.bfloat16)
    transfer = jnp.dot(flat, coupling, preferred_element_type=jnp.float32).reshape(shape)
    forcing = (wind_forcing * (1.0 - ice_flags.astype(jnp.float32)))[..., None]
    return advected + time_step * (forcing * advected + transfer - dissipation * energy * advected)


def neighbours(field):
    wide_x = extended(field, (("lon", 0),), 1, True)
    wide_y = extended(field, (("lat", 1),), 1, False)
    return (wide_x[:-2], wide_x[2:], wide_y[:, :-2], wide_y[:, 2:])


def on_device(spectrum, sea_mask, ice_flags, wind_forcing, group_speed, coupling):
    rows_here = spectrum.shape[1]
    rows = lax.axis_index("lat") * rows_here + jnp.arange(rows_here, dtype=jnp.int32)
    along_x, along_y = speed_tables(rows, rows_here * lax.axis_size("lat"), group_speed, DIRS)
    sea = sea_mask.astype(jnp.float32)[..., None]
    field = spectrum * sea
    for step in range(STEPS):
        west, east, south, north = neighbours(field)
        advected = upwind(field, west, east, south, north, along_x, along_y)
        field = sources(advected, wind_forcing, ice_flags, coupling) * sea
    return field


def solution(mesh):
    placed = (P("lon", "lat", None), P("lon", "lat"), P("lon", "lat"), P("lon", "lat"), P(), P())
    return jax.shard_map(
        on_device, mesh=mesh, in_specs=placed, out_specs=P("lon", "lat", None), check_vma=False
    )
```

profile of v0, /device:TPU:56, one launch (start us, length us, event | category | flops | bytes accessed | tf_op | source)
XLA Modules:
  0.0 117.7 jit_solution(2806012927057495896)
XLA Ops:
  0.8 1.6 %broadcast_multiply_fusion = f32[8,64,648]{2,1,0:T(8,128)S(1)} fusion(f32[8,64,648]{2,1,0:T(8,128)} %param.6, f32[8,64]{1,0:T(8,128)S(1)} %convert_element_type.44), kind=kLoop, calls=%fused_computation.80 | loop fusion | flops 331776 | bytes 2656256 | tf_op jit(solution)/shard_map/mul | solution.py:72
  3.0 1.9 %collective-permute-start.2 = (f32[8,1,648]{2,1,0:T(1,128)}, f32[8,1,648]{2,1,0:T(1,128)}, u32[]{:S(2)}, u32[]{:S(2)}) collective-permute-start(f32[8,1,648]{2,1,0:T(1,128)} %get-tuple-element.27), channel_id=1, source_target_pairs={{0,1},{1,2},{2,3},{3,4},{4,5},{5,6},{6,7},{7,8},{8,9},{9,10},{10,1... | collective-permute-start | bytes 62216 | tf_op jit(solution)/shard_map/ppermute | solution.py:23
  5.0 3.6 %collective-permute-start.3 = (f32[8,1,648]{2,1,0:T(1,128)}, f32[8,1,648]{2,1,0:T(1,128)}, u32[]{:S(2)}, u32[]{:S(2)}) collective-permute-start(f32[8,1,648]{2,1,0:T(1,128)} %get-tuple-element.28), channel_id=1, source_target_pairs={{1,0},{2,1},{3,2},{4,3},{5,4},{6,5},{7,6},{8,7},{9,8},{10,9},{11,1... | collective-permute-start | bytes 62216 | tf_op jit(solution)/shard_map/ppermute | solution.py:24
  9.3 7.9 %collective-permute-start = (f32[1,64,648]{2,1,0:T(8,128)}, f32[1,64,648]{2,1,0:T(8,128)S(1)}, u32[]{:S(2)}, u32[]{:S(2)}) collective-permute-start(f32[1,64,648]{2,1,0:T(8,128)} %get-tuple-element.25), channel_id=1, source_target_pairs={{0,48},{48,96},{96,144},{144,192},{192,240},{240,288},{288,336},{3... | collective-permute-start | bytes 497672 | tf_op jit(solution)/shard_map/ppermute | solution.py:23
  17.2 10.8 %collective-permute-start.1 = (f32[1,64,648]{2,1,0:T(8,128)S(1)}, f32[1,64,648]{2,1,0:T(8,128)S(1)}, u32[]{:S(2)}, u32[]{:S(2)}) collective-permute-start(f32[1,64,648]{2,1,0:T(8,128)S(1)} %get-tuple-element.26), channel_id=1, source_target_pairs={{48,0},{96,48},{144,96},{192,144},{240,192},{288,240},{336,288},{3... | collective-permute-start | bytes 497672 | tf_op jit(solution)/shard_map/ppermute | solution.py:24
  30.1 1.3 %subtract_multiply_fusion = f32[8,64]{1,0:T(8,128)} fusion(f32[8,64]{1,0:T(8,128)} %param.9, s32[8,64]{1,0:T(8,128)} %param.8), kind=kLoop, calls=%fused_computation.87 | loop fusion | flops 1536 | bytes 6144 | tf_op jit(solution)/shard_map/mul | solution.py:57
  32.2 1.4 %min.26 = f32[648]{0:T(1024)} reshape(f32[36,18]{1,0:T(8,128)} %get-tuple-element.32) | data formatting | bytes 5184 | tf_op jit(solution)/shard_map/min | solution.py:48
  33.7 5.2 %collective-permute-done.1 = f32[1,64,648]{2,1,0:T(8,128)S(1)} collective-permute-done((f32[1,64,648]{2,1,0:T(8,128)S(1)}, f32[1,64,648]{2,1,0:T(8,128)S(1)}, u32[]{:S(2)}, u32[]{:S(2)}) %collective-permute-start.1) | collective-permute-done | bytes 165920 | tf_op jit(solution)/shard_map/ppermute | solution.py:24
  38.9 1.8 %fusion.86 = (f32[8,64]{1,0:T(8,128)S(1)}, f32[8,64,648]{2,1,0:T(8,128)S(1)}) fusion(f32[8,64,648]{2,1,0:T(8,128)S(1)} %broadcast_multiply_fusion, f32[8,1,648]{2,1,0:T(1,128)} %collective-permute-done.3, f32[648]{0:T(1024)} %min.26, f32[8,1,648]{2,1,0:T(1,128)} %collective-permute-done.2, f32[648]{0:T(1024)S(1)} %max.26, ...), kind=kLoop, calls=%fused_computation.99 | loop fusion | flops 5639680 | bytes 3366464 | tf_op jit(solution)/shard_map/reduce_sum | solution.py:54
  41.8 5.3 %collective-permute-start.4 = (f32[1,64,648]{2,1,0:T(8,128)S(1)}, f32[1,64,648]{2,1,0:T(8,128)S(1)}, u32[]{:S(2)}, u32[]{:S(2)}) collective-permute-start(f32[1,64,648]{2,1,0:T(8,128)S(1)} %get-tuple-element.21), channel_id=1, source_target_pairs={{0,48},{48,96},{96,144},{144,192},{192,240},{240,288},{288,336},{3... | collective-permute-start | bytes 497672 | tf_op jit(solution)/shard_map/ppermute | solution.py:23
  47.1 7.1 %collective-permute-start.5 = (f32[1,64,648]{2,1,0:T(8,128)S(1)}, f32[1,64,648]{2,1,0:T(8,128)S(1)}, u32[]{:S(2)}, u32[]{:S(2)}) collective-permute-start(f32[1,64,648]{2,1,0:T(8,128)S(1)} %get-tuple-element.22), channel_id=1, source_target_pairs={{48,0},{96,48},{144,96},{192,144},{240,192},{288,240},{336,288},{3... | collective-permute-start | bytes 497672 | tf_op jit(solution)/shard_map/ppermute | solution.py:24
  54.3 1.9 %collective-permute-start.6 = (f32[8,1,648]{2,1,0:T(1,128)S(1)}, f32[8,1,648]{2,1,0:T(1,128)S(1)}, u32[]{:S(2)}, u32[]{:S(2)}) collective-permute-start(f32[8,1,648]{2,1,0:T(1,128)S(1)} %get-tuple-element.23), channel_id=1, source_target_pairs={{0,1},{1,2},{2,3},{3,4},{4,5},{5,6},{6,7},{7,8},{8,9},{9,10},{10,1... | collective-permute-start | bytes 62216 | tf_op jit(solution)/shard_map/ppermute | solution.py:23
  56.2 3.6 %collective-permute-start.7 = (f32[8,1,648]{2,1,0:T(1,128)S(1)}, f32[8,1,648]{2,1,0:T(1,128)S(1)}, u32[]{:S(2)}, u32[]{:S(2)}) collective-permute-start(f32[8,1,648]{2,1,0:T(1,128)S(1)} %get-tuple-element.24), channel_id=1, source_target_pairs={{1,0},{2,1},{3,2},{4,3},{5,4},{6,5},{7,6},{8,7},{9,8},{10,9},{11,1... | collective-permute-start | bytes 62216 | tf_op jit(solution)/shard_map/ppermute | solution.py:24
  59.9 1.5 %collective-permute-done.7 = f32[8,1,648]{2,1,0:T(1,128)S(1)} collective-permute-done((f32[8,1,648]{2,1,0:T(1,128)S(1)}, f32[8,1,648]{2,1,0:T(1,128)S(1)}, u32[]{:S(2)}, u32[]{:S(2)}) %collective-permute-start.7) | collective-permute-done | bytes 20768 | tf_op jit(solution)/shard_map/ppermute | solution.py:24
  61.4 1.5 %collective-permute-done.5 = f32[1,64,648]{2,1,0:T(8,128)S(1)} collective-permute-done((f32[1,64,648]{2,1,0:T(8,128)S(1)}, f32[1,64,648]{2,1,0:T(8,128)S(1)}, u32[]{:S(2)}, u32[]{:S(2)}) %collective-permute-start.5) | collective-permute-done | bytes 165920 | tf_op jit(solution)/shard_map/ppermute | solution.py:24
  62.9 1.1 fusion.84
  64.0 1.0 add_multiply_fusion.2
  65.1 3.7 %collective-permute-start.8 = (f32[1,64,648]{2,1,0:T(8,128)S(1)}, f32[1,64,648]{2,1,0:T(8,128)S(1)}, u32[]{:S(2)}, u32[]{:S(2)}) collective-permute-start(f32[1,64,648]{2,1,0:T(8,128)S(1)} %get-tuple-element.17), channel_id=1, source_target_pairs={{0,48},{48,96},{96,144},{144,192},{192,240},{240,288},{288,336},{3... | collective-permute-start | bytes 497672 | tf_op jit(solution)/shard_map/ppermute | solution.py:23
  68.8 7.3 %collective-permute-start.9 = (f32[1,64,648]{2,1,0:T(8,128)S(1)}, f32[1,64,648]{2,1,0:T(8,128)S(1)}, u32[]{:S(2)}, u32[]{:S(2)}) collective-permute-start(f32[1,64,648]{2,1,0:T(8,128)S(1)} %get-tuple-element.18), channel_id=1, source_target_pairs={{48,0},{96,48},{144,96},{192,144},{240,192},{288,240},{336,288},{3... | collective-permute-start | bytes 497672 | tf_op jit(solution)/shard_map/ppermute | solution.py:24
  76.1 2.9 %collective-permute-start.10 = (f32[8,1,648]{2,1,0:T(1,128)S(1)}, f32[8,1,648]{2,1,0:T(1,128)S(1)}, u32[]{:S(2)}, u32[]{:S(2)}) collective-permute-start(f32[8,1,648]{2,1,0:T(1,128)S(1)} %get-tuple-element.19), channel_id=1, source_target_pairs={{0,1},{1,2},{2,3},{3,4},{4,5},{5,6},{6,7},{7,8},{8,9},{9,10},{10,1... | collective-permute-start | bytes 62216 | tf_op jit(solution)/shard_map/ppermute | solution.py:23
  79.0 3.4 %collective-permute-start.11 = (f32[8,1,648]{2,1,0:T(1,128)S(1)}, f32[8,1,648]{2,1,0:T(1,128)S(1)}, u32[]{:S(2)}, u32[]{:S(2)}) collective-permute-start(f32[8,1,648]{2,1,0:T(1,128)S(1)} %get-tuple-element.20), channel_id=1, source_target_pairs={{1,0},{2,1},{3,2},{4,3},{5,4},{6,5},{7,6},{8,7},{9,8},{10,9},{11,1... | collective-permute-start | bytes 62216 | tf_op jit(solution)/shard_map/ppermute | solution.py:24
  82.4 1.5 %collective-permute-done.11 = f32[8,1,648]{2,1,0:T(1,128)S(1)} collective-permute-done((f32[8,1,648]{2,1,0:T(1,128)S(1)}, f32[8,1,648]{2,1,0:T(1,128)S(1)}, u32[]{:S(2)}, u32[]{:S(2)}) %collective-permute-start.11) | collective-permute-done | bytes 20768 | tf_op jit(solution)/shard_map/ppermute | solution.py:24
  83.9 5.5 %collective-permute-done.9 = f32[1,64,648]{2,1,0:T(8,128)S(1)} collective-permute-done((f32[1,64,648]{2,1,0:T(8,128)S(1)}, f32[1,64,648]{2,1,0:T(8,128)S(1)}, u32[]{:S(2)}, u32[]{:S(2)}) %collective-permute-start.9) | collective-permute-done | bytes 165920 | tf_op jit(solution)/shard_map/ppermute | solution.py:24
  89.3 1.1 fusion.82
  91.5 4.0 %collective-permute-start.12 = (f32[1,64,648]{2,1,0:T(8,128)S(1)}, f32[1,64,648]{2,1,0:T(8,128)S(1)}, u32[]{:S(2)}, u32[]{:S(2)}) collective-permute-start(f32[1,64,648]{2,1,0:T(8,128)S(1)} %get-tuple-element.13), channel_id=1, source_target_pairs={{0,48},{48,96},{96,144},{144,192},{192,240},{240,288},{288,336},{3... | collective-permute-start | bytes 497672 | tf_op jit(solution)/shard_map/ppermute | solution.py:23
  95.5 7.6 %collective-permute-start.13 = (f32[1,64,648]{2,1,0:T(8,128)S(1)}, f32[1,64,648]{2,1,0:T(8,128)S(1)}, u32[]{:S(2)}, u32[]{:S(2)}) collective-permute-start(f32[1,64,648]{2,1,0:T(8,128)S(1)} %get-tuple-element.14), channel_id=1, source_target_pairs={{48,0},{96,48},{144,96},{192,144},{240,192},{288,240},{336,288},{3... | collective-permute-start | bytes 497672 | tf_op jit(solution)/shard_map/ppermute | solution.py:24
  103.2 1.9 %collective-permute-start.14 = (f32[8,1,648]{2,1,0:T(1,128)S(1)}, f32[8,1,648]{2,1,0:T(1,128)S(1)}, u32[]{:S(2)}, u32[]{:S(2)}) collective-permute-start(f32[8,1,648]{2,1,0:T(1,128)S(1)} %get-tuple-element.15), channel_id=1, source_target_pairs={{0,1},{1,2},{2,3},{3,4},{4,5},{5,6},{6,7},{7,8},{8,9},{9,10},{10,1... | collective-permute-start | bytes 62216 | tf_op jit(solution)/shard_map/ppermute | solution.py:23
  105.1 3.6 %collective-permute-start.15 = (f32[8,1,648]{2,1,0:T(1,128)S(1)}, f32[8,1,648]{2,1,0:T(1,128)S(1)}, u32[]{:S(2)}, u32[]{:S(2)}) collective-permute-start(f32[8,1,648]{2,1,0:T(1,128)S(1)} %get-tuple-element.16), channel_id=1, source_target_pairs={{1,0},{2,1},{3,2},{4,3},{5,4},{6,5},{7,6},{8,7},{9,8},{10,9},{11,1... | collective-permute-start | bytes 62216 | tf_op jit(solution)/shard_map/ppermute | solution.py:24
  108.8 1.5 %collective-permute-done.15 = f32[8,1,648]{2,1,0:T(1,128)S(1)} collective-permute-done((f32[8,1,648]{2,1,0:T(1,128)S(1)}, f32[8,1,648]{2,1,0:T(1,128)S(1)}, u32[]{:S(2)}, u32[]{:S(2)}) %collective-permute-start.15) | collective-permute-done | bytes 20768 | tf_op jit(solution)/shard_map/ppermute | solution.py:24
  110.3 4.1 %collective-permute-done.12 = f32[1,64,648]{2,1,0:T(8,128)S(1)} collective-permute-done((f32[1,64,648]{2,1,0:T(8,128)S(1)}, f32[1,64,648]{2,1,0:T(8,128)S(1)}, u32[]{:S(2)}, u32[]{:S(2)}) %collective-permute-start.12) | collective-permute-done | bytes 165920 | tf_op jit(solution)/shard_map/ppermute | solution.py:23
  114.4 1.1 fusion.80
  115.5 2.1 %add_multiply_fusion = f32[8,64,648]{2,1,0:T(8,128)} fusion(f32[8,64,648]{2,1,0:T(8,128)S(1)} %get-tuple-element.6, f32[8,64]{1,0:T(8,128)S(1)} %broadcast_multiply_fusion.1, bf16[648,648]{1,0:T(8,128)(2,1)S(1)} %copy-done, f32[8,64]{1,0:T(8,128)S(1)} %copy-done.4, f32[8,64]{1,0:T(8,128)S(1)} %copy-done.3), kind=kOutput, calls=%fused_computation.64 | convolution fusion | flops 432635904 | bytes 3500160 | tf_op jit(solution)/shard_map/dot_general | solution.py:56
  (42 shorter events, 7.4 us)
Async XLA Ops:
  0.0 40.7 %copy-start = (bf16[648,648]{1,0:T(8,128)(2,1)S(1)}, bf16[648,648]{1,0:T(8,128)(2,1)}, u32[]{:S(2)}) copy-start(bf16[648,648]{1,0:T(8,128)(2,1)} %param.11) | copy-start | bytes 2519428
  0.8 1.6 %copy-start.2 = (f32[8,64]{1,0:T(8,128)}, f32[8,64]{1,0:T(8,128)S(1)}, u32[]{:S(2)}) copy-start(f32[8,64]{1,0:T(8,128)S(1)} %convert_element_type.44) | copy-start | bytes 6148
  0.8 27.8 %copy-start.5 = (f32[18]{0:T(128)S(1)}, f32[18]{0:T(128)}, u32[]{:S(2)}) copy-start(f32[18]{0:T(128)} %param.10) | copy-start | bytes 220
  3.0 30.6 %collective-permute-start.2 = (f32[8,1,648]{2,1,0:T(1,128)}, f32[8,1,648]{2,1,0:T(1,128)}, u32[]{:S(2)}, u32[]{:S(2)}) collective-permute-start(f32[8,1,648]{2,1,0:T(1,128)} %get-tuple-element.27), channel_id=1, source_target_pairs={{0,1},{1,2},{2,3},{3,4},{4,5},{5,6},{6,7},{7,8},{8,9},{9,10},{10,1... | collective-permute-start | bytes 62216 | tf_op jit(solution)/shard_map/ppermute | solution.py:23
  5.0 28.7 %collective-permute-start.3 = (f32[8,1,648]{2,1,0:T(1,128)}, f32[8,1,648]{2,1,0:T(1,128)}, u32[]{:S(2)}, u32[]{:S(2)}) collective-permute-start(f32[8,1,648]{2,1,0:T(1,128)} %get-tuple-element.28), channel_id=1, source_target_pairs={{1,0},{2,1},{3,2},{4,3},{5,4},{6,5},{7,6},{8,7},{9,8},{10,9},{11,1... | collective-permute-start | bytes 62216 | tf_op jit(solution)/shard_map/ppermute | solution.py:24
  9.3 24.4 %collective-permute-start = (f32[1,64,648]{2,1,0:T(8,128)}, f32[1,64,648]{2,1,0:T(8,128)S(1)}, u32[]{:S(2)}, u32[]{:S(2)}) collective-permute-start(f32[1,64,648]{2,1,0:T(8,128)} %get-tuple-element.25), channel_id=1, source_target_pairs={{0,48},{48,96},{96,144},{144,192},{192,240},{240,288},{288,336},{3... | collective-permute-start | bytes 497672 | tf_op jit(solution)/shard_map/ppermute | solution.py:23
  17.2 21.7 %collective-permute-start.1 = (f32[1,64,648]{2,1,0:T(8,128)S(1)}, f32[1,64,648]{2,1,0:T(8,128)S(1)}, u32[]{:S(2)}, u32[]{:S(2)}) collective-permute-start(f32[1,64,648]{2,1,0:T(8,128)S(1)} %get-tuple-element.26), channel_id=1, source_target_pairs={{48,0},{96,48},{144,96},{192,144},{240,192},{288,240},{336,288},{3... | collective-permute-start | bytes 497672 | tf_op jit(solution)/shard_map/ppermute | solution.py:24
  38.9 1.8 %copy-start.3 = (f32[8,64]{1,0:T(8,128)S(1)}, f32[8,64]{1,0:T(8,128)}, u32[]{:S(2)}) copy-start(f32[8,64]{1,0:T(8,128)} %copy-done.2) | copy-start | bytes 6148
  38.9 1.8 %copy-start.4 = (f32[8,64]{1,0:T(8,128)S(1)}, f32[8,64]{1,0:T(8,128)}, u32[]{:S(2)}) copy-start(f32[8,64]{1,0:T(8,128)} %subtract_multiply_fusion) | copy-start | bytes 6148
  40.7 22.1 %copy-start.1 = (f32[648]{0:T(1024)S(1)}, f32[648]{0:T(1024)}, u32[]{:S(2)}) copy-start(f32[648]{0:T(1024)} %min.26) | copy-start | bytes 7780
  41.8 19.5 %collective-permute-start.4 = (f32[1,64,648]{2,1,0:T(8,128)S(1)}, f32[1,64,648]{2,1,0:T(8,128)S(1)}, u32[]{:S(2)}, u32[]{:S(2)}) collective-permute-start(f32[1,64,648]{2,1,0:T(8,128)S(1)} %get-tuple-element.21), channel_id=1, source_target_pairs={{0,48},{48,96},{96,144},{144,192},{192,240},{240,288},{288,336},{3... | collective-permute-start | bytes 497672 | tf_op jit(solution)/shard_map/ppermute | solution.py:23
  47.1 15.8 %collective-permute-start.5 = (f32[1,64,648]{2,1,0:T(8,128)S(1)}, f32[1,64,648]{2,1,0:T(8,128)S(1)}, u32[]{:S(2)}, u32[]{:S(2)}) collective-permute-start(f32[1,64,648]{2,1,0:T(8,128)S(1)} %get-tuple-element.22), channel_id=1, source_target_pairs={{48,0},{96,48},{144,96},{192,144},{240,192},{288,240},{336,288},{3... | collective-permute-start | bytes 497672 | tf_op jit(solution)/shard_map/ppermute | solution.py:24
  54.3 5.6 %collective-permute-start.6 = (f32[8,1,648]{2,1,0:T(1,128)S(1)}, f32[8,1,648]{2,1,0:T(1,128)S(1)}, u32[]{:S(2)}, u32[]{:S(2)}) collective-permute-start(f32[8,1,648]{2,1,0:T(1,128)S(1)} %get-tuple-element.23), channel_id=1, source_target_pairs={{0,1},{1,2},{2,3},{3,4},{4,5},{5,6},{6,7},{7,8},{8,9},{9,10},{10,1... | collective-permute-start | bytes 62216 | tf_op jit(solution)/shard_map/ppermute | solution.py:23
  56.2 5.1 %collective-permute-start.7 = (f32[8,1,648]{2,1,0:T(1,128)S(1)}, f32[8,1,648]{2,1,0:T(1,128)S(1)}, u32[]{:S(2)}, u32[]{:S(2)}) collective-permute-start(f32[8,1,648]{2,1,0:T(1,128)S(1)} %get-tuple-element.24), channel_id=1, source_target_pairs={{1,0},{2,1},{3,2},{4,3},{5,4},{6,5},{7,6},{8,7},{9,8},{10,9},{11,1... | collective-permute-start | bytes 62216 | tf_op jit(solution)/shard_map/ppermute | solution.py:24
  65.1 18.8 %collective-permute-start.8 = (f32[1,64,648]{2,1,0:T(8,128)S(1)}, f32[1,64,648]{2,1,0:T(8,128)S(1)}, u32[]{:S(2)}, u32[]{:S(2)}) collective-permute-start(f32[1,64,648]{2,1,0:T(8,128)S(1)} %get-tuple-element.17), channel_id=1, source_target_pairs={{0,48},{48,96},{96,144},{144,192},{192,240},{240,288},{288,336},{3... | collective-permute-start | bytes 497672 | tf_op jit(solution)/shard_map/ppermute | solution.py:23
  68.8 20.6 %collective-permute-start.9 = (f32[1,64,648]{2,1,0:T(8,128)S(1)}, f32[1,64,648]{2,1,0:T(8,128)S(1)}, u32[]{:S(2)}, u32[]{:S(2)}) collective-permute-start(f32[1,64,648]{2,1,0:T(8,128)S(1)} %get-tuple-element.18), channel_id=1, source_target_pairs={{48,0},{96,48},{144,96},{192,144},{240,192},{288,240},{336,288},{3... | collective-permute-start | bytes 497672 | tf_op jit(solution)/shard_map/ppermute | solution.py:24
  76.1 6.3 %collective-permute-start.10 = (f32[8,1,648]{2,1,0:T(1,128)S(1)}, f32[8,1,648]{2,1,0:T(1,128)S(1)}, u32[]{:S(2)}, u32[]{:S(2)}) collective-permute-start(f32[8,1,648]{2,1,0:T(1,128)S(1)} %get-tuple-element.19), channel_id=1, source_target_pairs={{0,1},{1,2},{2,3},{3,4},{4,5},{5,6},{6,7},{7,8},{8,9},{9,10},{10,1... | collective-permute-start | bytes 62216 | tf_op jit(solution)/shard_map/ppermute | solution.py:23
  79.0 4.9 %collective-permute-start.11 = (f32[8,1,648]{2,1,0:T(1,128)S(1)}, f32[8,1,648]{2,1,0:T(1,128)S(1)}, u32[]{:S(2)}, u32[]{:S(2)}) collective-permute-start(f32[8,1,648]{2,1,0:T(1,128)S(1)} %get-tuple-element.20), channel_id=1, source_target_pairs={{1,0},{2,1},{3,2},{4,3},{5,4},{6,5},{7,6},{8,7},{9,8},{10,9},{11,1... | collective-permute-start | bytes 62216 | tf_op jit(solution)/shard_map/ppermute | solution.py:24
  91.5 22.8 %collective-permute-start.12 = (f32[1,64,648]{2,1,0:T(8,128)S(1)}, f32[1,64,648]{2,1,0:T(8,128)S(1)}, u32[]{:S(2)}, u32[]{:S(2)}) collective-permute-start(f32[1,64,648]{2,1,0:T(8,128)S(1)} %get-tuple-element.13), channel_id=1, source_target_pairs={{0,48},{48,96},{96,144},{144,192},{192,240},{240,288},{288,336},{3... | collective-permute-start | bytes 497672 | tf_op jit(solution)/shard_map/ppermute | solution.py:23
  95.5 18.8 %collective-permute-start.13 = (f32[1,64,648]{2,1,0:T(8,128)S(1)}, f32[1,64,648]{2,1,0:T(8,128)S(1)}, u32[]{:S(2)}, u32[]{:S(2)}) collective-permute-start(f32[1,64,648]{2,1,0:T(8,128)S(1)} %get-tuple-element.14), channel_id=1, source_target_pairs={{48,0},{96,48},{144,96},{192,144},{240,192},{288,240},{336,288},{3... | collective-permute-start | bytes 497672 | tf_op jit(solution)/shard_map/ppermute | solution.py:24
  103.2 5.6 %collective-permute-start.14 = (f32[8,1,648]{2,1,0:T(1,128)S(1)}, f32[8,1,648]{2,1,0:T(1,128)S(1)}, u32[]{:S(2)}, u32[]{:S(2)}) collective-permute-start(f32[8,1,648]{2,1,0:T(1,128)S(1)} %get-tuple-element.15), channel_id=1, source_target_pairs={{0,1},{1,2},{2,3},{3,4},{4,5},{5,6},{6,7},{7,8},{8,9},{9,10},{10,1... | collective-permute-start | bytes 62216 | tf_op jit(solution)/shard_map/ppermute | solution.py:23
  105.1 5.1 %collective-permute-start.15 = (f32[8,1,648]{2,1,0:T(1,128)S(1)}, f32[8,1,648]{2,1,0:T(1,128)S(1)}, u32[]{:S(2)}, u32[]{:S(2)}) collective-permute-start(f32[8,1,648]{2,1,0:T(1,128)S(1)} %get-tuple-element.16), channel_id=1, source_target_pairs={{1,0},{2,1},{3,2},{4,3},{5,4},{6,5},{7,6},{8,7},{9,8},{10,9},{11,1... | collective-permute-start | bytes 62216 | tf_op jit(solution)/shard_map/ppermute | solution.py:24
where the time goes:
time: 119 us; the launch traced here: 118 us
  starting transfers between devices  76.6 us (64%)
  waiting for transfers between devices  20.8 us (17%)
  other arithmetic  10.8 us (9%)
  matrix products  5.25 us (4%)
  local copies, waits for them, and re-layouts  3.92 us (3%)
    ppermute x8, starting transfers between devices, extended(): after = lax.ppermute(first, axis, down)  47.1 us
    ppermute x8, starting transfers between devices, extended(): before = lax.ppermute(last, axis, up)  29.4 us
    ppermute x8, waiting for transfers between devices, extended(): after = lax.ppermute(first, axis, down)  16.6 us
    dot_general x4, matrix products, sources(): jnp.dot(flat, coupling, preferred_element_type=jnp.float32).reshape(shape)  5.25 us
    reduce_sum x4, other arithmetic, sources(): energy = jnp.mean(advected, axis=-1, keepdims=True)  5.15 us
    ppermute x8, waiting for transfers between devices, extended(): before = lax.ppermute(last, axis, up)  4.14 us
  transfers between devices with their start and end apart: 16, of which 7 were waited for; matrix products, arithmetic and copies ran while one was open for 5% of the time, Pallas kernels for 0%

commit v1 on v0

v1 whole, which is shorter than its diff:
```python
import functools
import math

import jax
import jax.numpy as jnp
import numpy as np
from jax import lax
from jax.experimental import pallas as pl
from jax.experimental.pallas import tpu as pltpu
from jax.sharding import PartitionSpec as P

DIRS = 36
STEPS = 4
TIME_STEP = 0.2
DISSIPATION = 0.5
LANES = 128
TILES = 6
WIDE = TILES * LANES
CHUNK = 16
PAD = 8
ORDER = (0, 3, 1, 2)
MESH = pl.DeviceIdType.MESH


def direction_rows(freqs):
    theta = ((np.arange(DIRS, dtype=np.float32) + np.float32(0.5)) * np.float32(2.0 * math.pi / DIRS))
    rows = np.zeros((8, WIDE), np.float32)
    bins = DIRS * freqs
    rows[0, :bins] = np.repeat(np.abs(np.cos(theta)), freqs)
    rows[1, :bins] = np.repeat(np.abs(np.sin(theta)), freqs)
    rows[2, :bins] = np.tile(np.arange(freqs), DIRS)
    rows[2, bins:] = -1.0
    return rows


def kernel(
    sizes,
    spectrum, sea, ice, wind, speed, coupling, rows_in,
    out,
    raw, field, sea_v, ice_v, wind_v, speed_s, couple_raw, couple, rows_v,
    keep, along_x, along_y, share, gain, moved, rounded,
    send, recv,
    in_sem, lon_send, lon_recv, lat_send, lat_recv,
):
    n_lon, n_lat, bins, freqs = sizes
    cx, cy = spectrum.shape[0], spectrum.shape[1]
    chunks = cy // CHUNK
    lon, lat = lax.axis_index("lon"), lax.axis_index("lat")
    east, west = lax.rem(lon + 1, n_lon), lax.rem(lon + n_lon - 1, n_lon)
    has_south, has_north = lat > 0, lat < n_lat - 1
    lane = lax.broadcasted_iota(jnp.int32, (CHUNK, LANES), 1)

    columns = (0, cx - 1) + tuple(range(1, cx - 1))
    column_in = {i: pltpu.make_async_copy(spectrum.at[i], raw.at[i], in_sem.at[i]) for i in columns}
    small = [
        pltpu.make_async_copy(src, dst, in_sem.at[cx + n])
        for n, (src, dst) in enumerate(
            [(sea, sea_v), (ice, ice_v), (wind, wind_v), (speed, speed_s), (rows_in, rows_v)]
        )
    ]
    couple_in = pltpu.make_async_copy(coupling, couple_raw, in_sem.at[cx + 5])
    for copy in small:
        copy.start()
    for i in columns:
        column_in[i].start()
    couple_in.start()

    zero = jnp.zeros((PAD, WIDE), jnp.float32)
    for par in range(2):
        for i in range(cx):
            field[par, i, 0:PAD, :] = zero
            field[par, i, PAD + cy : PAD + cy + PAD, :] = zero

    barrier = pltpu.get_barrier_semaphore()
    pl.semaphore_signal(barrier, inc=1, device_id={"lon": east}, device_id_type=MESH)
    pl.semaphore_signal(barrier, inc=1, device_id={"lon": west}, device_id_type=MESH)

    @pl.when(has_south)
    def _():
        pl.semaphore_signal(barrier, inc=1, device_id={"lat": lat - 1}, device_id_type=MESH)

    @pl.when(has_north)
    def _():
        pl.semaphore_signal(barrier, inc=1, device_id={"lat": lat + 1}, device_id_type=MESH)

    for copy in small:
        copy.wait()
    speed_row = jnp.zeros((1, WIDE), jnp.float32)
    which = rows_v[2:3, :]
    for f in range(freqs):
        speed_row = jnp.where(which == f, speed_s[f], speed_row)
    scaled_x = 0.225 * (rows_v[0:1, :] * speed_row)
    scaled_y = 0.45 * (rows_v[1:2, :] * speed_row)
    row = (lat * cy + lax.broadcasted_iota(jnp.int32, (cy, LANES), 0)).astype(jnp.float32)
    phi = (-60.0 + 120.0 * (row + 0.5) / (cy * n_lat)) * (math.pi / 180.0)
    square = phi * phi
    cosine = jnp.full((cy, LANES), 1.0 / math.factorial(16), jnp.float32)
    for term in range(7, -1, -1):
        cosine = cosine * square + (-1.0) ** term / math.factorial(2 * term)
    inverse = 1.0 / cosine
    along_y[...] = jnp.broadcast_to(scaled_y, (8, WIDE))
    for k in range(TILES):
        cut = slice(k * LANES, (k + 1) * LANES)
        speed_x = inverse * scaled_x[:, cut]
        along_x[:, cut] = speed_x
        keep[:, cut] = 1.0 - speed_x - scaled_y[:, cut]

    sea_f = sea_v[...].astype(jnp.float32)
    forcing = wind_v[...] * (1.0 - ice_v[...].astype(jnp.float32))
    gain_t = jnp.transpose(sea_f * (1.0 + TIME_STEP * forcing))
    sea_t = jnp.transpose(sea_f)
    for i in range(cx):
        share[i] = TIME_STEP * jnp.broadcast_to(sea_t[:, i : i + 1], (cy, LANES))
        gain[i] = jnp.broadcast_to(gain_t[:, i : i + 1], (cy, LANES))

    def load_column(i):
        sea_i = jnp.broadcast_to(sea_t[:, i : i + 1], (cy, LANES))
        for k in range(TILES):
            cut = slice(k * LANES, (k + 1) * LANES)
            if (k + 1) * LANES <= bins:
                field[0, i, PAD : PAD + cy, cut] = raw[i, :, cut] * sea_i
            else:
                tail = bins - k * LANES
                last = raw[i, :, k * LANES : bins] * sea_i[:, :tail]
                field[0, i, PAD : PAD + cy, cut] = jnp.concatenate(
                    [last, jnp.zeros((cy, LANES - tail), jnp.float32)], axis=1
                )

    def lon_copy(side, par, c):
        return pltpu.make_async_remote_copy(
            src_ref=send.at[side, par, c],
            dst_ref=recv.at[side, par, c],
            send_sem=lon_send.at[side, par, c],
            recv_sem=lon_recv.at[side, par, c],
            device_id={"lon": west if side else east},
            device_id_type=MESH,
        )

    def lat_copy(side, par):
        if side == 0:
            src = field.at[par, :, PAD + cy - 1 : PAD + cy, 0 : 3 * LANES]
            dst = field.at[par, :, PAD - 1 : PAD, 0 : 3 * LANES]
        else:
            src = field.at[par, :, PAD : PAD + 1, 2 * LANES : WIDE]
            dst = field.at[par, :, PAD + cy : PAD + cy + 1, 2 * LANES : WIDE]
        return pltpu.make_async_remote_copy(
            src_ref=src,
            dst_ref=dst,
            send_sem=lat_send.at[side, par],
            recv_sem=lat_recv.at[side, par],
            device_id={"lat": lat - 1 if side else lat + 1},
            device_id_type=MESH,
        )

    def lat_start(par):
        @pl.when(has_north)
        def _():
            lat_copy(0, par).start()

        @pl.when(has_south)
        def _():
            lat_copy(1, par).start()

    def lat_wait_send(par):
        @pl.when(has_north)
        def _():
            lat_copy(0, par).wait_send()

        @pl.when(has_south)
        def _():
            lat_copy(1, par).wait_send()

    def lat_wait_recv(par):
        @pl.when(has_south)
        def _():
            lat_copy(0, par).wait_recv()

        @pl.when(has_north)
        def _():
            lat_copy(1, par).wait_recv()

    def pack_east(par, c, t):
        send[0, par, c, 0] = t[0]
        send[0, par, c, 1] = t[4]
        tail = pltpu.roll(t[5], 34, 1)
        send[0, par, c, 2] = jnp.where(lane < 34, t[1], jnp.where(lane < 102, tail, t[3]))

    def pack_west(par, c, t):
        send[1, par, c, 0] = t[2]
        send[1, par, c, 1] = jnp.where(lane < 34, t[3], t[1])
        send[1, par, c, 2] = t[3]

    def tile(par, i, r0, k):
        return field[par, i, PAD + r0 : PAD + r0 + CHUNK, k * LANES : (k + 1) * LANES]

    def advect(par, i, c):
        r0 = c * CHUNK
        if i == 0:
            a, b, m = recv[0, par, c, 0], recv[0, par, c, 1], recv[0, par, c, 2]
            from_west = {0: a, 1: m, 3: m, 4: b, 5: pltpu.roll(m, LANES - 34, 1)}
        else:
            from_west = {k: tile(par, i - 1, r0, k) for k in (0, 1, 3, 4, 5)}
        if i == cx - 1:
            a, b, m = recv[1, par, c, 0], recv[1, par, c, 1], recv[1, par, c, 2]
            from_east = {1: b, 2: a, 3: jnp.where(lane < 34, b, m)}
        else:
            from_east = {k: tile(par, i + 1, r0, k) for k in (1, 2, 3)}
        up_x = [
            from_west[0],
            jnp.where(lane < 34, from_west[1], from_east[1]),
            from_east[2],
            jnp.where(lane < 102, from_east[3], from_west[3]),
            from_west[4],
            from_west[5],
        ]
        out_tiles = []
        for k in range(TILES):
            rows = slice(r0, r0 + CHUNK)
            cut = slice(k * LANES, (k + 1) * LANES)
            south = tile(par, i, r0 - 1, k) if k <= 2 else None
            north = tile(par, i, r0 + 1, k) if k >= 2 else None
            up_y = south if north is None else north if south is None else jnp.where(lane < 68, south, north)
            speed_y = jnp.concatenate([along_y[:, cut]] * (CHUNK // 8), axis=0)
            out_tiles.append(
                tile(par, i, r0, k) * keep[rows, cut] + along_x[rows, cut] * up_x[k] + speed_y * up_y
            )
        return out_tiles

    def cell_gain(i, c, t):
        rows = slice(c * CHUNK, (c + 1) * CHUNK)
        total = jnp.sum((t[0] + t[1]) + (t[2] + t[3]) + (t[4] + t[5]), axis=1, keepdims=True)
        return gain[i, rows, :] - share[i, rows, :] * (total * (DISSIPATION / bins))

    def put(par, i, c, tiles, last):
        r0 = c * CHUNK
        for k in range(TILES):
            if not last:
                field[par, i, PAD + r0 : PAD + r0 + CHUNK, k * LANES : (k + 1) * LANES] = tiles[k]
            elif (k + 1) * LANES <= bins:
                out[i, r0 : r0 + CHUNK, k * LANES : (k + 1) * LANES] = tiles[k]
            else:
                out[i, r0 : r0 + CHUNK, k * LANES : bins] = tiles[k][:, : bins - k * LANES]

    def cells(par, blocks, last):
        gains = []
        for n, (i, c) in enumerate(blocks):
            t = advect(par, i, c)
            gains.append(cell_gain(i, c, t))
            for k in range(TILES):
                cut = slice(k * LANES, (k + 1) * LANES)
                moved[n * CHUNK : (n + 1) * CHUNK, cut] = t[k]
                rounded[n * CHUNK : (n + 1) * CHUNK, cut] = t[k].astype(jnp.bfloat16)
        height = len(blocks) * CHUNK
        transfer = jnp.dot(rounded[0:height, :], couple[...], preferred_element_type=jnp.float32)
        results = []
        for n, (i, c) in enumerate(blocks):
            part = share[i, c * CHUNK : (c + 1) * CHUNK, :]
            tiles = []
            for k in range(TILES):
                cut = slice(k * LANES, (k + 1) * LANES)
                rows = slice(n * CHUNK, (n + 1) * CHUNK)
                tiles.append(moved[rows, cut] * gains[n] + transfer[rows, cut] * part)
            put(1 - par, i, c, tiles, last)
            results.append(tiles)
        return results

    def step_body(n, last):
        par = lax.rem(n, 2)
        nxt = 1 - par
        if not last:
            @pl.when(n >= 1)
            def _():
                lat_wait_send(nxt)

        lat_wait_recv(par)
        for place, c in enumerate(ORDER):
            lon_copy(0, par, c).wait_recv()
            lon_copy(1, par, c).wait_recv()
            first, final = cells(par, [(0, c), (cx - 1, c)], last)
            if not last:
                @pl.when(n >= 1)
                def _():
                    lon_copy(0, nxt, c).wait_send()
                    lon_copy(1, nxt, c).wait_send()

                pack_east(nxt, c, final)
                pack_west(nxt, c, first)
                lon_copy(0, nxt, c).start()
                lon_copy(1, nxt, c).start()
            if place % 2 == 1:
                pair = (ORDER[place - 1], c)
                cells(par, [(i, b) for b in pair for i in range(1, cx - 1)], last)
                if place == 1 and not last:
                    lat_start(nxt)

    for i in columns[:2]:
        column_in[i].wait()
        load_column(i)
    for c in ORDER:
        pack_east(0, c, [tile(0, cx - 1, c * CHUNK, k) for k in range(TILES)])
        pack_west(0, c, [tile(0, 0, c * CHUNK, k) for k in range(TILES)])
    peers = 2 + jnp.minimum(lat, 1) + jnp.minimum(n_lat - 1 - lat, 1)
    pl.semaphore_wait(barrier, peers)

    for c in ORDER:
        lon_copy(0, 0, c).start()
        lon_copy(1, 0, c).start()
    for i in columns[2:]:
        column_in[i].wait()
        load_column(i)
    lat_start(0)
    couple_in.wait()
    couple[...] = jnp.zeros(couple.shape, couple.dtype)
    couple[0:bins, 0:bins] = couple_raw[...]

    def loop(n, carry):
        step_body(n, False)
        return carry

    lax.fori_loop(0, STEPS - 1, loop, 0)
    step_body(STEPS - 1, True)
    for par in range(2):
        lat_wait_send(par)
        for c in ORDER:
            lon_copy(0, par, c).wait_send()
            lon_copy(1, par, c).wait_send()


def on_device(n_lon, n_lat, spectrum, sea_mask, ice_flags, wind_forcing, group_speed, coupling):
    cx, cy, bins = spectrum.shape
    freqs = group_speed.shape[0]
    chunks = cy // CHUNK
    f32 = jnp.float32
    dma = pltpu.SemaphoreType.DMA
    scratch = [
        pltpu.VMEM((cx, cy, bins), f32),
        pltpu.VMEM((2, cx, cy + 2 * PAD, WIDE), f32),
        pltpu.VMEM((cx, cy), jnp.int32),
        pltpu.VMEM((cx, cy), jnp.int32),
        pltpu.VMEM((cx, cy), f32),
        pltpu.SMEM((freqs,), f32),
        pltpu.VMEM((bins, bins), jnp.bfloat16),
        pltpu.VMEM((WIDE, WIDE), jnp.bfloat16),
        pltpu.VMEM((8, WIDE), f32),
        pltpu.VMEM((cy, WIDE), f32),
        pltpu.VMEM((cy, WIDE), f32),
        pltpu.VMEM((8, WIDE), f32),
        pltpu.VMEM((cx, cy, LANES), f32),
        pltpu.VMEM((cx, cy, LANES), f32),
        pltpu.VMEM((2 * (cx - 2) * CHUNK, WIDE), f32),
        pltpu.VMEM((2 * (cx - 2) * CHUNK, WIDE), jnp.bfloat16),
        pltpu.VMEM((2, 2, chunks, 3, CHUNK, LANES), f32),
        pltpu.VMEM((2, 2, chunks, 3, CHUNK, LANES), f32),
        dma((cx + 6,)),
        dma((2, 2, chunks)),
        dma((2, 2, chunks)),
        dma((2, 2)),
        dma((2, 2)),
    ]
    anywhere = pl.BlockSpec(memory_space=pl.ANY)
    return pl.pallas_call(
        functools.partial(kernel, (n_lon, n_lat, bins, freqs)),
        out_shape=jax.ShapeDtypeStruct((cx, cy, bins), f32),
        in_specs=[anywhere] * 7,
        out_specs=pl.BlockSpec(memory_space=pltpu.VMEM),
        scratch_shapes=scratch,
        compiler_params=pltpu.CompilerParams(
            collective_id=0, has_side_effects=True, vmem_limit_bytes=63000 * 1024
        ),
    )(spectrum, sea_mask, ice_flags, wind_forcing, group_speed, coupling, jnp.asarray(direction_rows(freqs)))


def solution(mesh):
    placed = (P("lon", "lat", None), P("lon", "lat"), P("lon", "lat"), P("lon", "lat"), P(), P())
    return jax.shard_map(
        functools.partial(on_device, mesh.shape["lon"], mesh.shape["lat"]),
        mesh=mesh, in_specs=placed, out_specs=P("lon", "lat", None), check_vma=False,
    )
```

time: 119 us -> 54.8 us (0.46)
  starting transfers between devices: 76.6 us -> 0 us
  Pallas kernels: 0 us -> 52 us
  waiting for transfers between devices: 20.8 us -> 0 us
  other arithmetic: 10.8 us -> 0 us
  matrix products: 5.25 us -> 0 us
  local copies, waits for them, and re-layouts: 3.92 us -> 2.67 us
    ppermute x16 -> x0, starting transfers between devices: 76.6 us -> none  [the longest x8 47.1 us: extended(): after = lax.ppermute(first, axis, down)]
    pallas_call x0 -> x1, Pallas kernels: none -> 52 us  [on_device(): pl.pallas_call(functools.partial(kernel, (n_lon, n_lat, bins, freqs)), ou...]
    ppermute x16 -> x0, waiting for transfers between devices: 20.8 us -> none  [the longest x8 16.6 us: extended(): after = lax.ppermute(first, axis, down)]
    dot_general x4 -> x0, matrix products: 5.25 us -> none  [sources(): jnp.dot(flat, coupling, preferred_element_type=jnp.float32).reshape(shape)]
    reduce_sum x4 -> x0, other arithmetic: 5.15 us -> none  [sources(): energy = jnp.mean(advected, axis=-1, keepdims=True)]
    mul x6 -> x0, other arithmetic: 2.9 us -> none  [the longest x1 1.59 us: on_device(): field = spectrum * sea]
    unnamed x12 -> x1, local copies, waits for them, and re-layouts: 0.02 us -> 2.67 us
    slice x8 -> x0, local copies, waits for them, and re-layouts: 1.55 us -> none  [extended(): last = lax.slice_in_dim(value, length - width, length, axis=dim)]
  transfers between devices with their start and end apart: 16 -> 0, of which waited for: 7 -> 0; matrix products, arithmetic and copies ran while one was open for 5% -> 0% of each run, Pallas kernels for 0% -> 0%
where the time goes in v1:
time: 54.8 us; the launch traced here: 54.6 us
  Pallas kernels  52 us (95%)
  local copies, waits for them, and re-layouts  2.67 us (5%)
    pallas_call x1, Pallas kernels, on_device(): pl.pallas_call(functools.partial(kernel, (n_lon, n_lat, bins, freqs)), ou...  52 us
    unnamed x1, local copies, waits for them, and re-layouts  2.67 us

profile of v1, /device:TPU:56, one launch (start us, length us, event | category | flops | bytes accessed | tf_op | source)
XLA Modules:
  0.0 54.6 jit_solution(2976852522209685696)
XLA Ops:
  0.0 52.0 %shard_map.73 = f32[8,64,648]{2,1,0:T(8,128)} custom-call(f32[8,64,648]{2,1,0:T(8,128)} %spectrum.1, s32[8,64]{1,0:T(8,128)} %sea.1, s32[8,64]{1,0:T(8,128)} %ice.1, f32[8,64]{1,0:T(8,128)} %wind.1, f32[18]{0:T(128)} %speed.1, bf16[648,648]{1,0:T(8,128)(2,1)} %coupling.1, f32[8,768]{1,0:T(8,128)} %constant.2.clone.rows_in), custom_call_target="tpu_custom_call" | custom-call | tf_op jit(solution)/shard_map/pallas_call | solution.py:361
  52.0 2.7 %copy.9 = f32[8,64,648]{2,1,0:T(8,128)} copy(f32[8,64,648]{2,1,0:T(8,128)} %shard_map.73) | data formatting | bytes 2654208

commit v2 on v1

--- a/solution.py
+++ b/solution.py
@@ -17,6 +17,8 @@
 TILES = 6
 WIDE = TILES * LANES
 CHUNK = 16
+WIRE = 2 * CHUNK + 9
+DEPTH = 2
 PAD = 8
 ORDER = (0, 3, 1, 2)
 MESH = pl.DeviceIdType.MESH
@@ -49,69 +51,41 @@
     east, west = lax.rem(lon + 1, n_lon), lax.rem(lon + n_lon - 1, n_lon)
     has_south, has_north = lat > 0, lat < n_lat - 1
     lane = lax.broadcasted_iota(jnp.int32, (CHUNK, LANES), 1)
+    lane8, sub8 = lane[0:8], lax.broadcasted_iota(jnp.int32, (8, LANES), 0)
+
+    barrier = pltpu.get_barrier_semaphore()
+    pl.semaphore_signal(barrier, inc=1, device_id={"lon": east}, device_id_type=MESH)
+    pl.semaphore_signal(barrier, inc=1, device_id={"lon": west}, device_id_type=MESH)
+
+    @pl.when(has_south)
+    def _():
+        pl.semaphore_signal(barrier, inc=1, device_id={"lat": lat - 1}, device_id_type=MESH)
+
+    @pl.when(has_north)
+    def _():
+        pl.semaphore_signal(barrier, inc=1, device_id={"lat": lat + 1}, device_id_type=MESH)
 
     columns = (0, cx - 1) + tuple(range(1, cx - 1))
     column_in = {i: pltpu.make_async_copy(spectrum.at[i], raw.at[i], in_sem.at[i]) for i in columns}
-    small = [
+    sea_in, *small = [
         pltpu.make_async_copy(src, dst, in_sem.at[cx + n])
         for n, (src, dst) in enumerate(
             [(sea, sea_v), (ice, ice_v), (wind, wind_v), (speed, speed_s), (rows_in, rows_v)]
         )
     ]
     couple_in = pltpu.make_async_copy(coupling, couple_raw, in_sem.at[cx + 5])
+    sea_in.start()
+    for i in columns[:2]:
+        column_in[i].start()
     for copy in small:
         copy.start()
-    for i in columns:
+    for i in columns[2:]:
         column_in[i].start()
     couple_in.start()
 
-    zero = jnp.zeros((PAD, WIDE), jnp.float32)
-    for par in range(2):
-        for i in range(cx):
-            field[par, i, 0:PAD, :] = zero
-            field[par, i, PAD + cy : PAD + cy + PAD, :] = zero
-
-    barrier = pltpu.get_barrier_semaphore()
-    pl.semaphore_signal(barrier, inc=1, device_id={"lon": east}, device_id_type=MESH)
-    pl.semaphore_signal(barrier, inc=1, device_id={"lon": west}, device_id_type=MESH)
-
-    @pl.when(has_south)
-    def _():
-        pl.semaphore_signal(barrier, inc=1, device_id={"lat": lat - 1}, device_id_type=MESH)
-
-    @pl.when(has_north)
-    def _():
-        pl.semaphore_signal(barrier, inc=1, device_id={"lat": lat + 1}, device_id_type=MESH)
-
-    for copy in small:
-        copy.wait()
-    speed_row = jnp.zeros((1, WIDE), jnp.float32)
-    which = rows_v[2:3, :]
-    for f in range(freqs):
-        speed_row = jnp.where(which == f, speed_s[f], speed_row)
-    scaled_x = 0.225 * (rows_v[0:1, :] * speed_row)
-    scaled_y = 0.45 * (rows_v[1:2, :] * speed_row)
-    row = (lat * cy + lax.broadcasted_iota(jnp.int32, (cy, LANES), 0)).astype(jnp.float32)
-    phi = (-60.0 + 120.0 * (row + 0.5) / (cy * n_lat)) * (math.pi / 180.0)
-    square = phi * phi
-    cosine = jnp.full((cy, LANES), 1.0 / math.factorial(16), jnp.float32)
-    for term in range(7, -1, -1):
-        cosine = cosine * square + (-1.0) ** term / math.factorial(2 * term)
-    inverse = 1.0 / cosine
-    along_y[...] = jnp.broadcast_to(scaled_y, (8, WIDE))
-    for k in range(TILES):
-        cut = slice(k * LANES, (k + 1) * LANES)
-        speed_x = inverse * scaled_x[:, cut]
-        along_x[:, cut] = speed_x
-        keep[:, cut] = 1.0 - speed_x - scaled_y[:, cut]
-
+    sea_in.wait()
     sea_f = sea_v[...].astype(jnp.float32)
-    forcing = wind_v[...] * (1.0 - ice_v[...].astype(jnp.float32))
-    gain_t = jnp.transpose(sea_f * (1.0 + TIME_STEP * forcing))
     sea_t = jnp.transpose(sea_f)
-    for i in range(cx):
-        share[i] = TIME_STEP * jnp.broadcast_to(sea_t[:, i : i + 1], (cy, LANES))
-        gain[i] = jnp.broadcast_to(gain_t[:, i : i + 1], (cy, LANES))
 
     def load_column(i):
         sea_i = jnp.broadcast_to(sea_t[:, i : i + 1], (cy, LANES))
@@ -179,16 +153,77 @@
         def _():
             lat_copy(1, par).wait_recv()
 
+    def tables():
+        for copy in small:
+            copy.wait()
+        speed_row = jnp.zeros((1, WIDE), jnp.float32)
+        which = rows_v[2:3, :]
+        for f in range(freqs):
+            speed_row = jnp.where(which == f, speed_s[f], speed_row)
+        scaled_x = 0.225 * (rows_v[0:1, :] * speed_row)
+        scaled_y = 0.45 * (rows_v[1:2, :] * speed_row)
+        row = (lat * cy + lax.broadcasted_iota(jnp.int32, (cy, LANES), 0)).astype(jnp.float32)
+        phi = (-60.0 + 120.0 * (row + 0.5) / (cy * n_lat)) * (math.pi / 180.0)
+        square = phi * phi
+        cosine = jnp.full((cy, LANES), 1.0 / math.factorial(16), jnp.float32)
+        for term in range(7, -1, -1):
+            cosine = cosine * square + (-1.0) ** term / math.factorial(2 * term)
+        inverse = 1.0 / cosine
+        along_y[...] = jnp.broadcast_to(scaled_y, (8, WIDE))
+        for k in range(TILES):
+            cut = slice(k * LANES, (k + 1) * LANES)
+            speed_x = inverse * scaled_x[:, cut]
+            along_x[:, cut] = speed_x
+            keep[:, cut] = 1.0 - speed_x - scaled_y[:, cut]
+
+        forcing = wind_v[...] * (1.0 - ice_v[...].astype(jnp.float32))
+        gain_t = jnp.transpose(sea_f * (1.0 + TIME_STEP * forcing))
+        for i in range(cx):
+            share[i] = TIME_STEP * jnp.broadcast_to(sea_t[:, i : i + 1], (cy, LANES))
+            gain[i] = jnp.broadcast_to(gain_t[:, i : i + 1], (cy, LANES))
+
+    def squeeze(side, par, c, first, second, rest):
+        send[side, par, c, 0:CHUNK] = first
+        send[side, par, c, CHUNK : 2 * CHUNK] = second
+        low, high = rest[0:8], rest[8:16]
+        send[side, par, c, 2 * CHUNK : 2 * CHUNK + 8] = jnp.where(lane8 < 64, low, pltpu.roll(high, 64, 1))
+        line = jnp.zeros((8, LANES), jnp.float32)
+        for half, part in enumerate((low, high)):
+            part = jnp.where((lane8 >= 64) & (lane8 < 68), part, 0.0)
+            for r in range(8):
+                spot = 32 * half + 4 * r
+                line = line + jnp.where(sub8 == r, pltpu.roll(part, (64 + spot) % LANES, 1), 0.0)
+        send[side, par, c, 2 * CHUNK + 8 : 2 * CHUNK + 9] = jnp.sum(line, axis=0, keepdims=True)
+
+    def spread(side, par, c):
+        first = recv[side, par, c, 0:CHUNK]
+        second = recv[side, par, c, CHUNK : 2 * CHUNK]
+        both = recv[side, par, c, 2 * CHUNK : 2 * CHUNK + 8]
+        line = jnp.broadcast_to(recv[side, par, c, 2 * CHUNK + 8 : 2 * CHUNK + 9], (8, LANES))
+        parts = []
+        for half, body in enumerate((both, pltpu.roll(both, 64, 1))):
+            tail = line
+            for r in range(8):
+                spot = 32 * half + 4 * r
+                tail = jnp.where(sub8 == r, pltpu.roll(line, (64 - spot) % LANES, 1), tail)
+            parts.append(jnp.where(lane8 < 64, body, tail))
+        return first, second, jnp.concatenate(parts, axis=0)
+
     def pack_east(par, c, t):
-        send[0, par, c, 0] = t[0]
-        send[0, par, c, 1] = t[4]
-        tail = pltpu.roll(t[5], 34, 1)
-        send[0, par, c, 2] = jnp.where(lane < 34, t[1], jnp.where(lane < 102, tail, t[3]))
+        rest = jnp.where(lane < 34, t[1], jnp.where(lane < 102, pltpu.roll(t[5], 34, 1), t[3]))
+        squeeze(0, par, c, t[0], t[4], pltpu.roll(rest, 26, 1))
 
     def pack_west(par, c, t):
-        send[1, par, c, 0] = t[2]
-        send[1, par, c, 1] = jnp.where(lane < 34, t[3], t[1])
-        send[1, par, c, 2] = t[3]
+        squeeze(1, par, c, t[2], jnp.where(lane < 34, t[3], t[1]), pltpu.roll(t[3], LANES - 34, 1))
+
+    def unpack_east(par, c):
+        first, second, rest = spread(0, par, c)
+        mixed = pltpu.roll(rest, LANES - 26, 1)
+        return {0: first, 1: mixed, 3: mixed, 4: second, 5: pltpu.roll(rest, LANES - 60, 1)}
+
+    def unpack_west(par, c):
+        first, second, rest = spread(1, par, c)
+        return {1: second, 2: first, 3: jnp.where(lane < 34, second, pltpu.roll(rest, 34, 1))}
 
     def tile(par, i, r0, k):
         return field[par, i, PAD + r0 : PAD + r0 + CHUNK, k * LANES : (k + 1) * LANES]
@@ -196,13 +231,11 @@
     def advect(par, i, c):
         r0 = c * CHUNK
         if i == 0:
-            a, b, m = recv[0, par, c, 0], recv[0, par, c, 1], recv[0, par, c, 2]
-            from_west = {0: a, 1: m, 3: m, 4: b, 5: pltpu.roll(m, LANES - 34, 1)}
+            from_west = unpack_east(par, c)
         else:
             from_west = {k: tile(par, i - 1, r0, k) for k in (0, 1, 3, 4, 5)}
         if i == cx - 1:
-            a, b, m = recv[1, par, c, 0], recv[1, par, c, 1], recv[1, par, c, 2]
-            from_east = {1: b, 2: a, 3: jnp.where(lane < 34, b, m)}
+            from_east = unpack_west(par, c)
         else:
             from_east = {k: tile(par, i + 1, r0, k) for k in (1, 2, 3)}
         up_x = [
@@ -264,6 +297,15 @@
             results.append(tiles)
         return results
 
+    def pace(place, par):
+        back = place - DEPTH
+        which = par if back >= 0 else 1 - par
+        for side in range(2):
+            lon_copy(side, which, ORDER[back]).wait_send()
+
+    def inner(par, pair, last):
+        cells(par, [(i, b) for b in pair for i in range(1, cx - 1)], last)
+
     def step_body(n, last):
         par = lax.rem(n, 2)
         nxt = 1 - par
@@ -273,25 +315,24 @@
                 lat_wait_send(nxt)
 
         lat_wait_recv(par)
+        if last:
+            inner(par, ORDER[0:2], last)
+            inner(par, ORDER[2:4], last)
         for place, c in enumerate(ORDER):
             lon_copy(0, par, c).wait_recv()
             lon_copy(1, par, c).wait_recv()
             first, final = cells(par, [(0, c), (cx - 1, c)], last)
-            if not last:
-                @pl.when(n >= 1)
-                def _():
-                    lon_copy(0, nxt, c).wait_send()
-                    lon_copy(1, nxt, c).wait_send()
-
-                pack_east(nxt, c, final)
-                pack_west(nxt, c, first)
-                lon_copy(0, nxt, c).start()
-                lon_copy(1, nxt, c).start()
+            if last:
+                continue
+            pack_east(nxt, c, final)
+            pack_west(nxt, c, first)
             if place % 2 == 1:
-                pair = (ORDER[place - 1], c)
-                cells(par, [(i, b) for b in pair for i in range(1, cx - 1)], last)
-                if place == 1 and not last:
+                inner(par, ORDER[place - 1 : place + 1], last)
+                if place == 1:
                     lat_start(nxt)
+            pace(place, nxt)
+            lon_copy(0, nxt, c).start()
+            lon_copy(1, nxt, c).start()
 
     for i in columns[:2]:
         column_in[i].wait()
@@ -302,16 +343,37 @@
     peers = 2 + jnp.minimum(lat, 1) + jnp.minimum(n_lat - 1 - lat, 1)
     pl.semaphore_wait(barrier, peers)
 
-    for c in ORDER:
+    def rest_of_start():
+        for i in columns[2:]:
+            column_in[i].wait()
+            load_column(i)
+        lat_start(0)
+        zero = jnp.zeros((8, WIDE), jnp.float32)
+
+        @pl.when(lat == 0)
+        def _():
+            for par in range(2):
+                for i in range(cx):
+                    field[par, i, 0:PAD, :] = zero
+
+        @pl.when(lat == n_lat - 1)
+        def _():
+            for par in range(2):
+                for i in range(cx):
+                    field[par, i, PAD + cy : PAD + cy + PAD, :] = zero
+
+    def rest_of_tables():
+        couple_in.wait()
+        couple[...] = jnp.zeros(couple.shape, couple.dtype)
+        couple[0:bins, 0:bins] = couple_raw[...]
+
+    for place, c in enumerate(ORDER):
+        if place >= DEPTH:
+            pace(place, 0)
         lon_copy(0, 0, c).start()
         lon_copy(1, 0, c).start()
-    for i in columns[2:]:
-        column_in[i].wait()
-        load_column(i)
-    lat_start(0)
-    couple_in.wait()
-    couple[...] = jnp.zeros(couple.shape, couple.dtype)
-    couple[0:bins, 0:bins] = couple_raw[...]
+        if place < 3:
+            (rest_of_start, tables, rest_of_tables)[place]()
 
     def loop(n, carry):
         step_body(n, False)
@@ -321,9 +383,9 @@
     step_body(STEPS - 1, True)
     for par in range(2):
         lat_wait_send(par)
-        for c in ORDER:
-            lon_copy(0, par, c).wait_send()
-            lon_copy(1, par, c).wait_send()
+    for c in ORDER[len(ORDER) - DEPTH :]:
+        lon_copy(0, (STEPS - 1) % 2, c).wait_send()
+        lon_copy(1, (STEPS - 1) % 2, c).wait_send()
 
 
 def on_device(n_lon, n_lat, spectrum, sea_mask, ice_flags, wind_forcing, group_speed, coupling):
@@ -349,8 +411,8 @@
         pltpu.VMEM((cx, cy, LANES), f32),
         pltpu.VMEM((2 * (cx - 2) * CHUNK, WIDE), f32),
         pltpu.VMEM((2 * (cx - 2) * CHUNK, WIDE), jnp.bfloat16),
-        pltpu.VMEM((2, 2, chunks, 3, CHUNK, LANES), f32),
-        pltpu.VMEM((2, 2, chunks, 3, CHUNK, LANES), f32),
+        pltpu.VMEM((2, 2, chunks, WIRE, LANES), f32),
+        pltpu.VMEM((2, 2, chunks, WIRE, LANES), f32),
         dma((cx + 6,)),
         dma((2, 2, chunks)),
         dma((2, 2, chunks)),
@@ -360,7 +422,7 @@
     anywhere = pl.BlockSpec(memory_space=pl.ANY)
     return pl.pallas_call(
         functools.partial(kernel, (n_lon, n_lat, bins, freqs)),
-        out_shape=jax.ShapeDtypeStruct((cx, cy, bins), f32),
+        out_shape=pltpu.VMEM((cx, cy, bins), f32),
         in_specs=[anywhere] * 7,
         out_specs=pl.BlockSpec(memory_space=pltpu.VMEM),
         scratch_shapes=scratch,

time: 54.8 us -> 49.3 us (0.90)
  Pallas kernels: 52 us -> 48 us
  local copies, waits for them, and re-layouts: 2.67 us -> 1.15 us
    pallas_call x1, Pallas kernels: 52 us -> 48 us  [on_device(): pl.pallas_call(functools.partial(kernel, (n_lon, n_lat, bins, freqs)), ou...]
    unnamed x1, local copies, waits for them, and re-layouts: 2.67 us -> 1.15 us
where the time goes in v2:
time: 49.3 us; the launch traced here: 49.2 us
  Pallas kernels  48 us (97%)
  local copies, waits for them, and re-layouts  1.15 us (2%)
    pallas_call x1, Pallas kernels, on_device(): pl.pallas_call(functools.partial(kernel, (n_lon, n_lat, bins, freqs)), ou...  48 us
    unnamed x1, local copies, waits for them, and re-layouts  1.15 us

profile of v2, /device:TPU:56, one launch (start us, length us, event | category | flops | bytes accessed | tf_op | source)
XLA Modules:
  0.0 49.2 jit_solution(15729224107098093639)
XLA Ops:
  0.0 48.0 %shard_map.73 = f32[8,64,648]{2,1,0:T(8,128)S(1)} custom-call(f32[8,64,648]{2,1,0:T(8,128)} %spectrum.1, s32[8,64]{1,0:T(8,128)} %sea.1, s32[8,64]{1,0:T(8,128)} %ice.1, f32[8,64]{1,0:T(8,128)} %wind.1, f32[18]{0:T(128)} %speed.1, bf16[648,648]{1,0:T(8,128)(2,1)} %coupling.1, f32[8,768]{1,0:T(8,128)} %constant.2.clone.rows_in), custom_call_target="tpu_custom_call" | custom-call | tf_op jit(solution)/shard_map/pallas_call | solution.py:423
  48.0 1.1 %copy.9 = f32[8,64,648]{2,1,0:T(8,128)} copy(f32[8,64,648]{2,1,0:T(8,128)S(1)} %shard_map.73) | data formatting | bytes 2654208

commit v3 on v2

--- a/solution.py
+++ b/solution.py
@@ -17,7 +17,8 @@
 TILES = 6
 WIDE = TILES * LANES
 CHUNK = 16
-WIRE = 2 * CHUNK + 9
+BLOCK = 16
+WIRE = 2 * CHUNK + CHUNK // 2 + 1
 DEPTH = 2
 PAD = 8
 ORDER = (0, 3, 1, 2)
@@ -51,7 +52,10 @@
     east, west = lax.rem(lon + 1, n_lon), lax.rem(lon + n_lon - 1, n_lon)
     has_south, has_north = lat > 0, lat < n_lat - 1
     lane = lax.broadcasted_iota(jnp.int32, (CHUNK, LANES), 1)
-    lane8, sub8 = lane[0:8], lax.broadcasted_iota(jnp.int32, (8, LANES), 0)
+    sub = lax.broadcasted_iota(jnp.int32, (8, LANES), 0)
+    lane8 = lane[0:8]
+    free_lanes = ((lane8 >= 38) & (lane8 < 102), (lane8 < 34) | (lane8 >= 98))
+    lane_block = lax.broadcasted_iota(jnp.int32, (BLOCK, LANES), 1)
 
     barrier = pltpu.get_barrier_semaphore()
     pl.semaphore_signal(barrier, inc=1, device_id={"lon": east}, device_id_type=MESH)
@@ -182,129 +186,146 @@
             share[i] = TIME_STEP * jnp.broadcast_to(sea_t[:, i : i + 1], (cy, LANES))
             gain[i] = jnp.broadcast_to(gain_t[:, i : i + 1], (cy, LANES))
 
-    def squeeze(side, par, c, first, second, rest):
-        send[side, par, c, 0:CHUNK] = first
-        send[side, par, c, CHUNK : 2 * CHUNK] = second
-        low, high = rest[0:8], rest[8:16]
-        send[side, par, c, 2 * CHUNK : 2 * CHUNK + 8] = jnp.where(lane8 < 64, low, pltpu.roll(high, 64, 1))
-        line = jnp.zeros((8, LANES), jnp.float32)
-        for half, part in enumerate((low, high)):
-            part = jnp.where((lane8 >= 64) & (lane8 < 68), part, 0.0)
+    def fold(side, par, c, first, second, near, far, left, at):
+        send[side, par, c, 0:16] = first
+        send[side, par, c, 16:32] = second
+        send[side, par, c, 32:40] = jnp.where(free_lanes[side], far, near)
+        line = None
+        for half in range(2):
+            body = left[8 * half : 8 * half + 8]
+            rows = [pltpu.roll(body, (32 * half + 4 * r - at) % LANES, 1) for r in range(8)]
             for r in range(8):
                 spot = 32 * half + 4 * r
-                line = line + jnp.where(sub8 == r, pltpu.roll(part, (64 + spot) % LANES, 1), 0.0)
-        send[side, par, c, 2 * CHUNK + 8 : 2 * CHUNK + 9] = jnp.sum(line, axis=0, keepdims=True)
-
-    def spread(side, par, c):
-        first = recv[side, par, c, 0:CHUNK]
-        second = recv[side, par, c, CHUNK : 2 * CHUNK]
-        both = recv[side, par, c, 2 * CHUNK : 2 * CHUNK + 8]
-        line = jnp.broadcast_to(recv[side, par, c, 2 * CHUNK + 8 : 2 * CHUNK + 9], (8, LANES))
-        parts = []
-        for half, body in enumerate((both, pltpu.roll(both, 64, 1))):
-            tail = line
-            for r in range(8):
-                spot = 32 * half + 4 * r
-                tail = jnp.where(sub8 == r, pltpu.roll(line, (64 - spot) % LANES, 1), tail)
-            parts.append(jnp.where(lane8 < 64, body, tail))
-        return first, second, jnp.concatenate(parts, axis=0)
+                pick = (sub == r) & (lane8 >= spot) & (lane8 < spot + 4)
+                line = jnp.where(pick, rows[r], 0.0 if line is None else line)
+        send[side, par, c, 40:41] = jnp.sum(line, axis=0, keepdims=True)
+
+    def unfold(side, par, c, at):
+        body = recv[side, par, c, 32:40]
+        line = jnp.broadcast_to(recv[side, par, c, 40:41], (8, LANES))
+        rest, left = jnp.concatenate([body, pltpu.roll(body, 64, 1)], axis=0), []
+        for half in range(2):
+            rows = [pltpu.roll(line, (at - 32 * half - 4 * r) % LANES, 1) for r in range(8)]
+            tail = rows[0]
+            for r in range(1, 8):
+                tail = jnp.where(sub == r, rows[r], tail)
+            left.append(tail)
+        return recv[side, par, c, 0:16], recv[side, par, c, 16:32], rest, jnp.concatenate(left, axis=0)
 
     def pack_east(par, c, t):
-        rest = jnp.where(lane < 34, t[1], jnp.where(lane < 102, pltpu.roll(t[5], 34, 1), t[3]))
-        squeeze(0, par, c, t[0], t[4], pltpu.roll(rest, 26, 1))
+        low, high = slice(0, 8), slice(8, 16)
+        near = jnp.where(lane8 < 34, t[1][low], jnp.where(lane8 < 38, pltpu.roll(t[5][low], 34, 1), t[3][low]))
+        mixed = jnp.where(lane8 < 34, t[1][high], t[3][high])
+        far = jnp.where((lane8 >= 98) & (lane8 < 102), pltpu.roll(t[5][high], 98, 1), pltpu.roll(mixed, 64, 1))
+        fold(0, par, c, t[0], t[4], near, far, t[5], 4)
 
     def pack_west(par, c, t):
-        squeeze(1, par, c, t[2], jnp.where(lane < 34, t[3], t[1]), pltpu.roll(t[3], LANES - 34, 1))
+        second = jnp.where(lane < 34, t[3], t[1])
+        fold(1, par, c, t[2], second, t[3][0:8], pltpu.roll(t[3][8:16], 64, 1), t[3], 98)
 
     def unpack_east(par, c):
-        first, second, rest = spread(0, par, c)
-        mixed = pltpu.roll(rest, LANES - 26, 1)
-        return {0: first, 1: mixed, 3: mixed, 4: second, 5: pltpu.roll(rest, LANES - 60, 1)}
+        first, second, rest, left = unfold(0, par, c, 4)
+        body = recv[0, par, c, 32:40]
+        four = jnp.concatenate([pltpu.roll(body, LANES - 34, 1), pltpu.roll(body, LANES - 98, 1)], axis=0)
+        return {0: first, 1: rest, 3: rest, 4: second, 5: jnp.where(lane < 4, four, left)}
 
     def unpack_west(par, c):
-        first, second, rest = spread(1, par, c)
-        return {1: second, 2: first, 3: jnp.where(lane < 34, second, pltpu.roll(rest, 34, 1))}
-
-    def tile(par, i, r0, k):
-        return field[par, i, PAD + r0 : PAD + r0 + CHUNK, k * LANES : (k + 1) * LANES]
-
-    def advect(par, i, c):
-        r0 = c * CHUNK
+        first, second, rest, left = unfold(1, par, c, 98)
+        return {1: second, 2: first, 3: jnp.where(lane < 34, second, jnp.where(lane < 98, rest, left))}
+
+    def tile(par, i, r0, rows, k):
+        return field[par, i, PAD + r0 : PAD + r0 + rows, k * LANES : (k + 1) * LANES]
+
+    def advect(par, i, r0, rows):
+        at = lane if rows == CHUNK else lane_block
         if i == 0:
-            from_west = unpack_east(par, c)
+            from_west = unpack_east(par, r0 // CHUNK)
         else:
-            from_west = {k: tile(par, i - 1, r0, k) for k in (0, 1, 3, 4, 5)}
+            from_west = {k: tile(par, i - 1, r0, rows, k) for k in (0, 1, 3, 4, 5)}
         if i == cx - 1:
-            from_east = unpack_west(par, c)
+            from_east = unpack_west(par, r0 // CHUNK)
         else:
-            from_east = {k: tile(par, i + 1, r0, k) for k in (1, 2, 3)}
+            from_east = {k: tile(par, i + 1, r0, rows, k) for k in (1, 2, 3)}
         up_x = [
             from_west[0],
-            jnp.where(lane < 34, from_west[1], from_east[1]),
+            jnp.where(at < 34, from_west[1], from_east[1]),
             from_east[2],
-            jnp.where(lane < 102, from_east[3], from_west[3]),
+            jnp.where(at < 102, from_east[3], from_west[3]),
             from_west[4],
             from_west[5],
         ]
         out_tiles = []
         for k in range(TILES):
-            rows = slice(r0, r0 + CHUNK)
+            span = slice(r0, r0 + rows)
             cut = slice(k * LANES, (k + 1) * LANES)
-            south = tile(par, i, r0 - 1, k) if k <= 2 else None
-            north = tile(par, i, r0 + 1, k) if k >= 2 else None
-            up_y = south if north is None else north if south is None else jnp.where(lane < 68, south, north)
-            speed_y = jnp.concatenate([along_y[:, cut]] * (CHUNK // 8), axis=0)
+            south = tile(par, i, r0 - 1, rows, k) if k <= 2 else None
+            north = tile(par, i, r0 + 1, rows, k) if k >= 2 else None
+            up_y = south if north is None else north if south is None else jnp.where(at < 68, south, north)
+            speed_y = jnp.concatenate([along_y[:, cut]] * (rows // 8), axis=0)
             out_tiles.append(
-                tile(par, i, r0, k) * keep[rows, cut] + along_x[rows, cut] * up_x[k] + speed_y * up_y
+                tile(par, i, r0, rows, k) * keep[span, cut] + along_x[span, cut] * up_x[k] + speed_y * up_y
             )
         return out_tiles
 
-    def cell_gain(i, c, t):
-        rows = slice(c * CHUNK, (c + 1) * CHUNK)
+    def cell_gain(i, r0, rows, t):
+        span = slice(r0, r0 + rows)
         total = jnp.sum((t[0] + t[1]) + (t[2] + t[3]) + (t[4] + t[5]), axis=1, keepdims=True)
-        return gain[i, rows, :] - share[i, rows, :] * (total * (DISSIPATION / bins))
-
-    def put(par, i, c, tiles, last):
-        r0 = c * CHUNK
+        return gain[i, span, :] - share[i, span, :] * (total * (DISSIPATION / bins))
+
+    def put(par, i, r0, rows, tiles, last):
         for k in range(TILES):
             if not last:
-                field[par, i, PAD + r0 : PAD + r0 + CHUNK, k * LANES : (k + 1) * LANES] = tiles[k]
+                field[par, i, PAD + r0 : PAD + r0 + rows, k * LANES : (k + 1) * LANES] = tiles[k]
             elif (k + 1) * LANES <= bins:
-                out[i, r0 : r0 + CHUNK, k * LANES : (k + 1) * LANES] = tiles[k]
+                out[i, r0 : r0 + rows, k * LANES : (k + 1) * LANES] = tiles[k]
             else:
-                out[i, r0 : r0 + CHUNK, k * LANES : bins] = tiles[k][:, : bins - k * LANES]
-
-    def cells(par, blocks, last):
+                out[i, r0 : r0 + rows, k * LANES : bins] = tiles[k][:, : bins - k * LANES]
+
+    def edges(par, c, last):
+        r0 = c * CHUNK
+        both = [advect(par, i, r0, CHUNK) for i in (0, cx - 1)]
+        gains = [cell_gain(i, r0, CHUNK, t) for i, t in zip((0, cx - 1), both)]
+        for k in range(TILES):
+            pair = jnp.concatenate([both[0][k], both[1][k]], axis=0)
+            rounded[0 : 2 * CHUNK, k * LANES : (k + 1) * LANES] = pair.astype(jnp.bfloat16)
+        transfer = jnp.dot(rounded[0 : 2 * CHUNK, :], couple[...], preferred_element_type=jnp.float32)
+        results = []
+        for n, i in enumerate((0, cx - 1)):
+            part = share[i, r0 : r0 + CHUNK, :]
+            lines = slice(n * CHUNK, (n + 1) * CHUNK)
+            tiles = [
+                both[n][k] * gains[n] + transfer[lines, k * LANES : (k + 1) * LANES] * part for k in range(TILES)
+            ]
+            put(1 - par, i, r0, CHUNK, tiles, last)
+            results.append(tiles)
+        return results
+
+    def inside(par, blocks, last):
+        spots = [(i, b * BLOCK) for b in blocks for i in range(1, cx - 1)]
         gains = []
-        for n, (i, c) in enumerate(blocks):
-            t = advect(par, i, c)
-            gains.append(cell_gain(i, c, t))
+        for n, (i, r0) in enumerate(spots):
+            t = advect(par, i, r0, BLOCK)
+            gains.append(cell_gain(i, r0, BLOCK, t))
             for k in range(TILES):
                 cut = slice(k * LANES, (k + 1) * LANES)
-                moved[n * CHUNK : (n + 1) * CHUNK, cut] = t[k]
-                rounded[n * CHUNK : (n + 1) * CHUNK, cut] = t[k].astype(jnp.bfloat16)
-        height = len(blocks) * CHUNK
+                moved[n * BLOCK : (n + 1) * BLOCK, cut] = t[k]
+                rounded[n * BLOCK : (n + 1) * BLOCK, cut] = t[k].astype(jnp.bfloat16)
+        height = len(spots) * BLOCK
         transfer = jnp.dot(rounded[0:height, :], couple[...], preferred_element_type=jnp.float32)
-        results = []
-        for n, (i, c) in enumerate(blocks):
-            part = share[i, c * CHUNK : (c + 1) * CHUNK, :]
+        for n, (i, r0) in enumerate(spots):
+            part = share[i, r0 : r0 + BLOCK, :]
             tiles = []
             for k in range(TILES):
                 cut = slice(k * LANES, (k + 1) * LANES)
-                rows = slice(n * CHUNK, (n + 1) * CHUNK)
-                tiles.append(moved[rows, cut] * gains[n] + transfer[rows, cut] * part)
-            put(1 - par, i, c, tiles, last)
-            results.append(tiles)
-        return results
+                lines = slice(n * BLOCK, (n + 1) * BLOCK)
+                tiles.append(moved[lines, cut] * gains[n] + transfer[lines, cut] * part)
+            put(1 - par, i, r0, BLOCK, tiles, last)
 
     def pace(place, par):
         back = place - DEPTH
         which = par if back >= 0 else 1 - par
         for side in range(2):
             lon_copy(side, which, ORDER[back]).wait_send()
-
-    def inner(par, pair, last):
-        cells(par, [(i, b) for b in pair for i in range(1, cx - 1)], last)
 
     def step_body(n, last):
         par = lax.rem(n, 2)
@@ -315,31 +336,31 @@
                 lat_wait_send(nxt)
 
         lat_wait_recv(par)
+        inside(par, (0, 3), last)
         if last:
-            inner(par, ORDER[0:2], last)
-            inner(par, ORDER[2:4], last)
+            inside(par, (1, 2), last)
         for place, c in enumerate(ORDER):
             lon_copy(0, par, c).wait_recv()
             lon_copy(1, par, c).wait_recv()
-            first, final = cells(par, [(0, c), (cx - 1, c)], last)
+            first, final = edges(par, c, last)
             if last:
                 continue
             pack_east(nxt, c, final)
             pack_west(nxt, c, first)
-            if place % 2 == 1:
-                inner(par, ORDER[place - 1 : place + 1], last)
-                if place == 1:
-                    lat_start(nxt)
             pace(place, nxt)
             lon_copy(0, nxt, c).start()
             lon_copy(1, nxt, c).start()
+            if place == 1:
+                lat_start(nxt)
+        if not last:
+            inside(par, (1, 2), last)
 
     for i in columns[:2]:
         column_in[i].wait()
         load_column(i)
     for c in ORDER:
-        pack_east(0, c, [tile(0, cx - 1, c * CHUNK, k) for k in range(TILES)])
-        pack_west(0, c, [tile(0, 0, c * CHUNK, k) for k in range(TILES)])
+        pack_east(0, c, [tile(0, cx - 1, c * CHUNK, CHUNK, k) for k in range(TILES)])
+        pack_west(0, c, [tile(0, 0, c * CHUNK, CHUNK, k) for k in range(TILES)])
     peers = 2 + jnp.minimum(lat, 1) + jnp.minimum(n_lat - 1 - lat, 1)
     pl.semaphore_wait(barrier, peers)
 
@@ -372,8 +393,8 @@
             pace(place, 0)
         lon_copy(0, 0, c).start()
         lon_copy(1, 0, c).start()
-        if place < 3:
-            (rest_of_start, tables, rest_of_tables)[place]()
+        if DEPTH - 1 <= place < DEPTH + 2:
+            (rest_of_start, tables, rest_of_tables)[place - DEPTH + 1]()
 
     def loop(n, carry):
         step_body(n, False)
@@ -409,8 +430,8 @@
         pltpu.VMEM((8, WIDE), f32),
         pltpu.VMEM((cx, cy, LANES), f32),
         pltpu.VMEM((cx, cy, LANES), f32),
-        pltpu.VMEM((2 * (cx - 2) * CHUNK, WIDE), f32),
-        pltpu.VMEM((2 * (cx - 2) * CHUNK, WIDE), jnp.bfloat16),
+        pltpu.VMEM((2 * (cx - 2) * BLOCK, WIDE), f32),
+        pltpu.VMEM((2 * (cx - 2) * BLOCK, WIDE), jnp.bfloat16),
         pltpu.VMEM((2, 2, chunks, WIRE, LANES), f32),
         pltpu.VMEM((2, 2, chunks, WIRE, LANES), f32),
         dma((cx + 6,)),

time: 49.3 us -> 48.7 us (0.988)
  Pallas kernels: 48 us -> 47.3 us
    pallas_call x1, Pallas kernels: 48 us -> 47.3 us  [on_device(): pl.pallas_call(functools.partial(kernel, (n_lon, n_lat, bins, freqs)), ou...]
where the time goes in v3:
time: 48.7 us; the launch traced here: 48.5 us
  Pallas kernels  47.3 us (97%)
  local copies, waits for them, and re-layouts  1.15 us (2%)
    pallas_call x1, Pallas kernels, on_device(): pl.pallas_call(functools.partial(kernel, (n_lon, n_lat, bins, freqs)), ou...  47.3 us
    unnamed x1, local copies, waits for them, and re-layouts  1.15 us

profile of v3, /device:TPU:56, one launch (start us, length us, event | category | flops | bytes accessed | tf_op | source)
XLA Modules:
  0.0 48.5 jit_solution(4002373783305439856)
XLA Ops:
  0.0 47.3 %shard_map.73 = f32[8,64,648]{2,1,0:T(8,128)S(1)} custom-call(f32[8,64,648]{2,1,0:T(8,128)} %spectrum.1, s32[8,64]{1,0:T(8,128)} %sea.1, s32[8,64]{1,0:T(8,128)} %ice.1, f32[8,64]{1,0:T(8,128)} %wind.1, f32[18]{0:T(128)} %speed.1, bf16[648,648]{1,0:T(8,128)(2,1)} %coupling.1, f32[8,768]{1,0:T(8,128)} %constant.2.clone.rows_in), custom_call_target="tpu_custom_call" | custom-call | tf_op jit(solution)/shard_map/pallas_call | solution.py:444
  47.3 1.1 %copy.9 = f32[8,64,648]{2,1,0:T(8,128)} copy(f32[8,64,648]{2,1,0:T(8,128)S(1)} %shard_map.73) | data formatting | bytes 2654208

commit v4 on v3

--- a/solution.py
+++ b/solution.py
@@ -106,8 +106,8 @@
 
     def lon_copy(side, par, c):
         return pltpu.make_async_remote_copy(
-            src_ref=send.at[side, par, c],
-            dst_ref=recv.at[side, par, c],
+            src_ref=send.at[side, par, c, 0:WIRE],
+            dst_ref=recv.at[side, par, c, 0:WIRE],
             send_sem=lon_send.at[side, par, c],
             recv_sem=lon_recv.at[side, par, c],
             device_id={"lon": west if side else east},
@@ -432,8 +432,8 @@
         pltpu.VMEM((cx, cy, LANES), f32),
         pltpu.VMEM((2 * (cx - 2) * BLOCK, WIDE), f32),
         pltpu.VMEM((2 * (cx - 2) * BLOCK, WIDE), jnp.bfloat16),
-        pltpu.VMEM((2, 2, chunks, WIRE, LANES), f32),
-        pltpu.VMEM((2, 2, chunks, WIRE, LANES), f32),
+        pltpu.VMEM((2, 2, chunks, WIRE + 7, LANES), f32),
+        pltpu.VMEM((2, 2, chunks, WIRE + 7, LANES), f32),
         dma((cx + 6,)),
         dma((2, 2, chunks)),
         dma((2, 2, chunks)),

time: 48.7 us -> 48.7 us (level)
  no operation moved by 1% of the time
where the time goes in v4:
time: 48.7 us; the launch traced here: 48.5 us
  Pallas kernels  47.3 us (97%)
  local copies, waits for them, and re-layouts  1.15 us (2%)
    pallas_call x1, Pallas kernels, on_device(): pl.pallas_call(functools.partial(kernel, (n_lon, n_lat, bins, freqs)), ou...  47.3 us
    unnamed x1, local copies, waits for them, and re-layouts  1.15 us

profile of v4, /device:TPU:56, one launch (start us, length us, event | category | flops | bytes accessed | tf_op | source)
XLA Modules:
  0.0 48.5 jit_solution(4002373783305439856)
XLA Ops:
  0.0 47.3 %shard_map.73 = f32[8,64,648]{2,1,0:T(8,128)S(1)} custom-call(f32[8,64,648]{2,1,0:T(8,128)} %spectrum.1, s32[8,64]{1,0:T(8,128)} %sea.1, s32[8,64]{1,0:T(8,128)} %ice.1, f32[8,64]{1,0:T(8,128)} %wind.1, f32[18]{0:T(128)} %speed.1, bf16[648,648]{1,0:T(8,128)(2,1)} %coupling.1, f32[8,768]{1,0:T(8,128)} %constant.2.clone.rows_in), custom_call_target="tpu_custom_call" | custom-call | tf_op jit(solution)/shard_map/pallas_call | solution.py:444
  47.3 1.1 %copy.9 = f32[8,64,648]{2,1,0:T(8,128)} copy(f32[8,64,648]{2,1,0:T(8,128)S(1)} %shard_map.73) | data formatting | bytes 2654208
